TPU v7x, 32 devices: a whole 2x2x4 slice. The times are simulated.
32 devices in a mesh: sx: 4 (over x, core), sy: 2 (over y), px: 4 (over z).
Axes of the slice: x: 2, y: 2, z: 4, core: 2. Of those that a mesh axis runs over, the one named last changes fastest.
Arguments:
- patterns: bfloat16 [64, 64, 9216], P('sx', 'sy', 'px'), may hold values from -6 to 6
- basis: bfloat16 [9216, 256], P('px', ('sx', 'sy')), may hold values from -0.375 to 0.375
- valid: int32 [64, 64], P('sx', 'sy'), may hold values 0 or 1
- strength: float32 [64, 64], P('sx', 'sy'), may hold values from 0.25 to 2
Outputs:
- denoised: bfloat16 [64, 64, 9216], P('sx', 'sy', 'px')
Inputs may be any that keep to these rules, and one draw needn't show every extreme that they name: `valid`: 1 marks an on-sample scan position, 0 an off-sample one.
All inputs are finite; a program needn't handle non-finite values. No bound on the sum of `valid` on one device may be relied on, other than what follows from the above.
Results may differ from a plain program's by a relative error of at most 0.0089.
Values may be sent and summed in bfloat16 or wider, within the bound.
No kernel may reach another device: no remote copies, remote signals or barrier semaphores. Data moves between devices by JAX's collectives and lax.ppermute only.
A program may use at most 64 MiB of HBM per device.

v0:
```python
import jax
import jax.numpy as jnp
from jax import lax
from jax.sharding import PartitionSpec as P

PIX = 9216
RADIUS = 3


def extended(array, sides, width):
    for axis, dim in sides:
        count, length = (lax.axis_size(axis), array.shape[dim])
        up = [(i, (i + 1) % count) for i in range(count - 1)]
        down = [(j, i) for i, j in up]
        last = lax.slice_in_dim(array, length - width, length, axis=dim)
        initial = lax.slice_in_dim(array, 0, width, axis=dim)
        before = lax.ppermute(last, axis, up)
        after = lax.ppermute(initial, axis, down)
        array = jnp.concatenate([before, array, after], axis=dim)
    return array


def neighbour_steps():
    steps = []
    for row_step in range(-RADIUS, RADIUS + 1):
        for col_step in range(-RADIUS, RADIUS + 1):
            if row_step != 0 or col_step != 0:
                steps.append((row_step, col_step))
    return steps


def squared_gaps(center, padded):
    rows, cols = (center.shape[0], center.shape[1])
    gaps = []
    for row_step, col_step in neighbour_steps():
        other = padded[
            RADIUS + row_step : RADIUS + row_step + rows,
            RADIUS + col_step : RADIUS + col_step + cols,
        ]
        differ = center - other
        gaps.append(jnp.sum(differ * differ, axis=-1))
    return jnp.stack(gaps)


def blend(center, padded, mask_pad, gaps, strength):
    rows, cols = (center.shape[0], center.shape[1])
    factor = 1.0 / (2.0 * PIX * strength)
    numerator = center
    total = jnp.ones((rows, cols), jnp.float32)
    for index, (row_step, col_step) in enumerate(neighbour_steps()):
        other = padded[
            RADIUS + row_step : RADIUS + row_step + rows,
            RADIUS + col_step : RADIUS + col_step + cols,
        ]
        mask_other = mask_pad[
            RADIUS + row_step : RADIUS + row_step + rows,
            RADIUS + col_step : RADIUS + col_step + cols,
        ]
        weight = mask_other * jnp.exp(-gaps[index] * factor)
        numerator = numerator + weight[:, :, None] * other
        total = total + weight
    return numerator / total[:, :, None]


def extend(coeffs, mask_full):
    return (
        extended(coeffs, (("sx", 0), ("sy", 1)), RADIUS),
        extended(mask_full, (("sx", 0), ("sy", 1)), RADIUS),
    )


def on_device(patterns, basis, valid, strength):
    cells_x, cells_y, pixels = patterns.shape
    flat = patterns.reshape(cells_x * cells_y, pixels)
    whole_basis = lax.all_gather(basis, ("sx", "sy"), axis=1, tiled=True)
    partial_value = jnp.dot(flat, whole_basis, preferred_element_type=jnp.float32)
    partial_value = partial_value.reshape(cells_x, cells_y, partial_value.shape[1])
    mask_full = valid.astype(jnp.float32)
    coeffs = lax.psum(partial_value, "px")
    padded, mask_pad = extend(coeffs, mask_full)
    gaps = squared_gaps(coeffs, padded)
    average = blend(coeffs, padded, mask_pad, gaps, strength).astype(jnp.bfloat16)
    avg_flat = average.reshape(cells_x * cells_y, average.shape[2])
    rebuilt = lax.dot_general(
        avg_flat, whole_basis, (((1,), (1,)), ((), ())), preferred_element_type=jnp.float32
    )
    return rebuilt.astype(jnp.bfloat16).reshape(cells_x, cells_y, pixels)


def solution(mesh):
    return jax.shard_map(
        on_device,
        mesh=mesh,
        in_specs=(P("sx", "sy", "px"), P("px", ("sx", "sy")), P("sx", "sy"), P("sx", "sy")),
        out_specs=P("sx", "sy", "px"),
        check_vma=False,
    )
```

profile of v0, /device:TPU:1, one launch (start us, length us, event | category | flops | bytes accessed | tf_op | source)
XLA Modules:
  0.0 117.6 jit_solution(7627593339896749223)
XLA Ops:
  6.5 0.0 copy-start
  6.5 0.0 all-gather.2.cloned.1.call-start
  6.5 0.7 all-gather.2.cloned.1.call-update
  7.3 0.0 copy-start.4
  7.3 0.0 all-reduce.2.cloned.1.call-start
  7.3 28.3 %all-gather.2.cloned.1.call-done = bf16[2304,256]{0,1:T(8,128)(2,1)} async-done(((bf16[2304,32]{0,1:T(8,128)(2,1)}), bf16[2304,256]{0,1:T(8,128)(2,1)}) %all-gather.2.cloned.1.call-update) | async-done | bytes 1179664 | tf_op jit(solution)/shard_map/all_gather | solution.py:75
  35.6 0.0 copy-done
  35.6 2.9 %fusion = f32[16,32,256]{2,1,0:T(8,128)} fusion(bf16[16,32,2304]{2,1,0:T(8,128)(2,1)S(1)} %copy-done, bf16[2304,256]{0,1:T(8,128)(2,1)} %all-gather.2.cloned.1.call-done), kind=kOutput, calls=%fused_computation.81 | convolution fusion | flops 603979776 | bytes 4063232 | tf_op jit(solution)/shard_map/dot_general | solution.py:76
  38.5 0.0 all-reduce.2.cloned.1.call-update
  38.5 0.0 copy-done.4
  38.6 3.3 %collective-permute-start = (f32[3,32]{1,0:T(4,128)S(1)}, f32[3,32]{1,0:T(4,128)S(1)}, u32[]{:S(2)}, u32[]{:S(2)}) collective-permute-start(f32[3,32]{1,0:T(4,128)S(1)} %get-tuple-element.124), channel_id=1, source_target_pairs={{0,8},{8,16},{16,24},{1,9},{9,17},{17,25},{2,10},{10,18},{18,26},{... | collective-permute-start | bytes 1160 | tf_op jit(solution)/shard_map/ppermute | solution.py:17
  41.8 1.9 %collective-permute-start.1 = (f32[3,32]{1,0:T(4,128)S(1)}, f32[3,32]{1,0:T(4,128)S(1)}, u32[]{:S(2)}, u32[]{:S(2)}) collective-permute-start(f32[3,32]{1,0:T(4,128)S(1)} %get-tuple-element.125), channel_id=1, source_target_pairs={{8,0},{16,8},{24,16},{9,1},{17,9},{25,17},{10,2},{18,10},{26,18},{... | collective-permute-start | bytes 1160 | tf_op jit(solution)/shard_map/ppermute | solution.py:18
  43.8 0.0 collective-permute-done
  43.8 3.4 %collective-permute-done.1 = f32[3,32]{1,0:T(4,128)S(1)} collective-permute-done((f32[3,32]{1,0:T(4,128)S(1)}, f32[3,32]{1,0:T(4,128)S(1)}, u32[]{:S(2)}, u32[]{:S(2)}) %collective-permute-start.1) | collective-permute-done | bytes 416 | tf_op jit(solution)/shard_map/ppermute | solution.py:18
  47.1 28.8 %all-reduce.2.cloned.1.call-done = f32[16,32,256]{2,1,0:T(8,128)} async-done(((f32[16,32,256]{2,1,0:T(8,128)}), f32[16,32,256]{2,1,0:T(8,128)}) %all-reduce.2.cloned.1.call-update) | async-done | bytes 524304 | tf_op jit(solution)/shard_map/psum | solution.py:79
  76.0 0.0 copy-start.1
  76.0 1.0 fusion.59
  77.0 4.6 %collective-permute-start.3 = (f32[3,32,256]{2,1,0:T(8,128)S(1)}, f32[3,32,256]{2,1,0:T(8,128)S(1)}, u32[]{:S(2)}, u32[]{:S(2)}) collective-permute-start(f32[3,32,256]{2,1,0:T(8,128)S(1)} %get-tuple-element.116), channel_id=1, source_target_pairs={{0,8},{8,16},{16,24},{1,9},{9,17},{17,25},{2,10},{10,18},{18,26},{... | collective-permute-start | bytes 294920 | tf_op jit(solution)/shard_map/ppermute | solution.py:17
  81.6 0.1 fusion.60
  81.7 3.1 %collective-permute-start.2 = (f32[22,3]{1,0:T(8,128)S(1)}, f32[22,3]{1,0:T(8,128)S(1)}, u32[]{:S(2)}, u32[]{:S(2)}) collective-permute-start(f32[22,3]{1,0:T(8,128)S(1)} %get-tuple-element.123), channel_id=1, source_target_pairs={{0,4},{1,5},{2,6},{3,7},{8,12},{9,13},{10,14},{11,15},{16,20},{17,... | collective-permute-start | bytes 800 | tf_op jit(solution)/shard_map/ppermute | solution.py:17
  84.7 1.3 %collective-permute-start.6 = (f32[22,3]{1,0:T(8,128)S(1)}, f32[22,3]{1,0:T(8,128)S(1)}, u32[]{:S(2)}, u32[]{:S(2)}) collective-permute-start(f32[22,3]{1,0:T(8,128)S(1)} %get-tuple-element.122), channel_id=1, source_target_pairs={{4,0},{5,1},{6,2},{7,3},{12,8},{13,9},{14,10},{15,11},{20,16},{21,... | collective-permute-start | bytes 800 | tf_op jit(solution)/shard_map/ppermute | solution.py:18
  86.0 1.9 %collective-permute-start.4 = (f32[3,32,256]{2,1,0:T(8,128)S(1)}, f32[3,32,256]{2,1,0:T(8,128)S(1)}, u32[]{:S(2)}, u32[]{:S(2)}) collective-permute-start(f32[3,32,256]{2,1,0:T(8,128)S(1)} %get-tuple-element.117), channel_id=1, source_target_pairs={{8,0},{16,8},{24,16},{9,1},{17,9},{25,17},{10,2},{18,10},{26,18},{... | collective-permute-start | bytes 294920 | tf_op jit(solution)/shard_map/ppermute | solution.py:18
  88.0 0.0 collective-permute-done.3
  88.0 1.2 constant_dynamic-update-slice_fusion.1
  89.2 2.8 %collective-permute-done.4 = f32[3,32,256]{2,1,0:T(8,128)S(1)} collective-permute-done((f32[3,32,256]{2,1,0:T(8,128)S(1)}, f32[3,32,256]{2,1,0:T(8,128)S(1)}, u32[]{:S(2)}, u32[]{:S(2)}) %collective-permute-start.4) | collective-permute-done | bytes 98336 | tf_op jit(solution)/shard_map/ppermute | solution.py:18
  92.0 1.3 %collective-permute-start.7 = (f32[22,3,256]{2,1,0:T(4,128)S(1)}, f32[22,3,256]{2,1,0:T(4,128)S(1)}, u32[]{:S(2)}, u32[]{:S(2)}) collective-permute-start(f32[22,3,256]{2,1,0:T(4,128)S(1)} %get-tuple-element.111), channel_id=1, source_target_pairs={{4,0},{5,1},{6,2},{7,3},{12,8},{13,9},{14,10},{15,11},{20,16},{21,... | collective-permute-start | bytes 202760 | tf_op jit(solution)/shard_map/ppermute | solution.py:18
  93.3 0.0 collective-permute-done.2
  93.3 0.0 collective-permute-done.6
  93.4 0.1 pad_maximum_fusion.3
  93.4 4.0 %collective-permute-start.5 = (f32[22,3,256]{2,1,0:T(4,128)S(1)}, f32[22,3,256]{2,1,0:T(4,128)S(1)}, u32[]{:S(2)}, u32[]{:S(2)}) collective-permute-start(f32[22,3,256]{2,1,0:T(4,128)S(1)} %get-tuple-element.112), channel_id=1, source_target_pairs={{0,4},{1,5},{2,6},{3,7},{8,12},{9,13},{10,14},{11,15},{16,20},{17,... | collective-permute-start | bytes 202760 | tf_op jit(solution)/shard_map/ppermute | solution.py:17
  97.4 0.0 collective-permute-done.7
  97.4 0.0 copy-done.1
  97.4 1.0 multiply_reduce_fusion.42
  98.4 1.0 multiply_reduce_fusion.43
  99.4 0.0 collective-permute-done.5
  99.4 1.1 multiply_reduce_fusion.46
  100.6 1.1 multiply_reduce_fusion.47
  101.7 0.0 copy-start.3
  101.7 1.2 %multiply_reduce_fusion.45 = (f32[16,32]{1,0:T(8,128)S(1)}, f32[16,32]{1,0:T(8,128)S(1)}, f32[16,32]{1,0:T(8,128)S(1)}, f32[16,32]{1,0:T(8,128)S(1)}, f32[16,32]...) fusion(f32[16,32,256]{2,1,0:T(8,128)S(1)} %copy-done.1, ...), kind=kLoop, calls=%fused_computation.171 | loop fusion | flops 5498880 | bytes 4550656 | tf_op jit(solution)/shard_map/reduce_sum | solution.py:41
  102.9 0.0 copy-done.3
  102.9 0.2 add_add_fusion
  103.1 0.0 copy-start.2
  103.1 5.4 %divide_convert_fusion = bf16[16,32,256]{2,1,0:T(8,128)(2,1)S(1)} fusion(f32[16,32,256]{2,1,0:T(8,128)S(1)} %copy-done.1, f32[19,32,256]{2,1,0:T(8,128)S(1)} %constant_dynamic-update-slice_fusion.5, f32[19,32,256]{2,1,0:T(8,128)S(1)} %get-tuple-element.115, f32[22,32,256]{2,1,0:T(8,128)S(1)} %constant_dynamic-update-slice_fusion, ...), kind=kLoop, calls=%fused_computation.125 | loop fusion | flops 18350080 | bytes 4888576 | tf_op jit(solution)/shard_map/convert_element_type | solution.py:82
  108.6 0.0 copy-done.2
  108.6 2.2 %convolution_convert_fusion = bf16[512,2304]{1,0:T(8,128)(2,1)} fusion(bf16[512,256]{1,0:T(8,128)(2,1)S(1)} %bitcast.8, bf16[2304,256]{0,1:T(8,128)(2,1)S(1)} %copy-done.2), kind=kOutput, calls=%fused_computation.40 | convolution fusion | flops 605159424 | bytes 3801088 | tf_op jit(solution)/shard_map/dot_general | solution.py:84
  (7 shorter events, 0.1 us)
Async XLA Ops:
  6.5 29.1 %copy-start = (bf16[16,32,2304]{2,1,0:T(8,128)(2,1)S(1)}, bf16[16,32,2304]{2,1,0:T(8,128)(2,1)}, u32[]{:S(2)}) copy-start(bf16[16,32,2304]{2,1,0:T(8,128)(2,1)} %param.4) | copy-start | bytes 7077892
  6.5 29.1 %all-gather.2.cloned.1.call-start = ((), (), s32[]{:S(2)}) async-start(), calls=%async_computation | async-start | bytes 1327104 | tf_op jit(solution)/shard_map/all_gather | solution.py:75
  7.3 31.3 %copy-start.4 = (s32[16,32]{1,0:T(8,128)S(1)}, s32[16,32]{1,0:T(8,128)}, u32[]{:S(2)}) copy-start(s32[16,32]{1,0:T(8,128)} %param.6) | copy-start | bytes 6148
  7.3 68.7 %all-reduce.2.cloned.1.call-start = ((), (), s32[]{:S(2)}) async-start(), calls=%async_computation.1 | async-start | bytes 1048576 | tf_op jit(solution)/shard_map/psum | solution.py:79
  38.6 5.2 %collective-permute-start = (f32[3,32]{1,0:T(4,128)S(1)}, f32[3,32]{1,0:T(4,128)S(1)}, u32[]{:S(2)}, u32[]{:S(2)}) collective-permute-start(f32[3,32]{1,0:T(4,128)S(1)} %get-tuple-element.124), channel_id=1, source_target_pairs={{0,8},{8,16},{16,24},{1,9},{9,17},{17,25},{2,10},{10,18},{18,26},{... | collective-permute-start | bytes 1160 | tf_op jit(solution)/shard_map/ppermute | solution.py:17
  41.8 5.3 %collective-permute-start.1 = (f32[3,32]{1,0:T(4,128)S(1)}, f32[3,32]{1,0:T(4,128)S(1)}, u32[]{:S(2)}, u32[]{:S(2)}) collective-permute-start(f32[3,32]{1,0:T(4,128)S(1)} %get-tuple-element.125), channel_id=1, source_target_pairs={{8,0},{16,8},{24,16},{9,1},{17,9},{25,17},{10,2},{18,10},{26,18},{... | collective-permute-start | bytes 1160 | tf_op jit(solution)/shard_map/ppermute | solution.py:18
  76.0 21.5 %copy-start.1 = (f32[16,32,256]{2,1,0:T(8,128)S(1)}, f32[16,32,256]{2,1,0:T(8,128)}, u32[]{:S(2)}) copy-start(f32[16,32,256]{2,1,0:T(8,128)} %all-reduce.2.cloned.1.call-done) | copy-start | bytes 1572868
  77.0 11.0 %collective-permute-start.3 = (f32[3,32,256]{2,1,0:T(8,128)S(1)}, f32[3,32,256]{2,1,0:T(8,128)S(1)}, u32[]{:S(2)}, u32[]{:S(2)}) collective-permute-start(f32[3,32,256]{2,1,0:T(8,128)S(1)} %get-tuple-element.116), channel_id=1, source_target_pairs={{0,8},{8,16},{16,24},{1,9},{9,17},{17,25},{2,10},{10,18},{18,26},{... | collective-permute-start | bytes 294920 | tf_op jit(solution)/shard_map/ppermute | solution.py:17
  81.7 11.7 %collective-permute-start.2 = (f32[22,3]{1,0:T(8,128)S(1)}, f32[22,3]{1,0:T(8,128)S(1)}, u32[]{:S(2)}, u32[]{:S(2)}) collective-permute-start(f32[22,3]{1,0:T(8,128)S(1)} %get-tuple-element.123), channel_id=1, source_target_pairs={{0,4},{1,5},{2,6},{3,7},{8,12},{9,13},{10,14},{11,15},{16,20},{17,... | collective-permute-start | bytes 800 | tf_op jit(solution)/shard_map/ppermute | solution.py:17
  84.7 8.6 %collective-permute-start.6 = (f32[22,3]{1,0:T(8,128)S(1)}, f32[22,3]{1,0:T(8,128)S(1)}, u32[]{:S(2)}, u32[]{:S(2)}) collective-permute-start(f32[22,3]{1,0:T(8,128)S(1)} %get-tuple-element.122), channel_id=1, source_target_pairs={{4,0},{5,1},{6,2},{7,3},{12,8},{13,9},{14,10},{15,11},{20,16},{21,... | collective-permute-start | bytes 800 | tf_op jit(solution)/shard_map/ppermute | solution.py:18
  86.0 5.9 %collective-permute-start.4 = (f32[3,32,256]{2,1,0:T(8,128)S(1)}, f32[3,32,256]{2,1,0:T(8,128)S(1)}, u32[]{:S(2)}, u32[]{:S(2)}) collective-permute-start(f32[3,32,256]{2,1,0:T(8,128)S(1)} %get-tuple-element.117), channel_id=1, source_target_pairs={{8,0},{16,8},{24,16},{9,1},{17,9},{25,17},{10,2},{18,10},{26,18},{... | collective-permute-start | bytes 294920 | tf_op jit(solution)/shard_map/ppermute | solution.py:18
  92.0 5.4 %collective-permute-start.7 = (f32[22,3,256]{2,1,0:T(4,128)S(1)}, f32[22,3,256]{2,1,0:T(4,128)S(1)}, u32[]{:S(2)}, u32[]{:S(2)}) collective-permute-start(f32[22,3,256]{2,1,0:T(4,128)S(1)} %get-tuple-element.111), channel_id=1, source_target_pairs={{4,0},{5,1},{6,2},{7,3},{12,8},{13,9},{14,10},{15,11},{20,16},{21,... | collective-permute-start | bytes 202760 | tf_op jit(solution)/shard_map/ppermute | solution.py:18
  93.4 6.0 %collective-permute-start.5 = (f32[22,3,256]{2,1,0:T(4,128)S(1)}, f32[22,3,256]{2,1,0:T(4,128)S(1)}, u32[]{:S(2)}, u32[]{:S(2)}) collective-permute-start(f32[22,3,256]{2,1,0:T(4,128)S(1)} %get-tuple-element.112), channel_id=1, source_target_pairs={{0,4},{1,5},{2,6},{3,7},{8,12},{9,13},{10,14},{11,15},{16,20},{17,... | collective-permute-start | bytes 202760 | tf_op jit(solution)/shard_map/ppermute | solution.py:17
  101.7 1.2 %copy-start.3 = (f32[16,32]{1,0:T(8,128)S(1)}, f32[16,32]{1,0:T(8,128)}, u32[]{:S(2)}) copy-start(f32[16,32]{1,0:T(8,128)} %param.7) | copy-start | bytes 6148
  103.1 5.5 %copy-start.2 = (bf16[2304,256]{0,1:T(8,128)(2,1)S(1)}, bf16[2304,256]{0,1:T(8,128)(2,1)}, u32[]{:S(2)}) copy-start(bf16[2304,256]{0,1:T(8,128)(2,1)} %all-gather.2.cloned.1.call-done) | copy-start | bytes 3538948
Sparse Core Ops, SparseCore 0:
  9.2 26.3 all-gather.1
  38.6 37.2 all-reduce.1
where the time goes:
time: 118 us
  waiting for transfers between devices  64.1 us (54%)
  starting transfers between devices  21.4 us (18%)
  between operations  13.7 us (12%)
  other arithmetic  11.1 us (9%)
  matrix products  5.06 us (4%)
  local copies, waits for them, and re-layouts  2.33 us (2%)
    psum x1, waiting for transfers between devices, on_device(): coeffs = lax.psum(partial_value, 'px')  28.8 us
    all_gather x1, waiting for transfers between devices, on_device(): whole_basis = lax.all_gather(basis, ('sx', 'sy'), axis=1, tiled=True)  28.3 us
    ppermute x4, starting transfers between devices, extended(): before = lax.ppermute(last, axis, up)  14.9 us
    ppermute x4, starting transfers between devices, extended(): after = lax.ppermute(initial, axis, down)  6.43 us
    ppermute x4, waiting for transfers between devices, extended(): after = lax.ppermute(initial, axis, down)  6.18 us
    convert_element_type x1, other arithmetic, on_device(): blend(coeffs, padded, mask_pad, gaps, strength).astype(jnp.bfloat16)  5.44 us
    reduce_sum x5, other arithmetic, squared_gaps(): gaps.append(jnp.sum(differ * differ, axis=-1))  5.39 us
    dot_general x1, matrix products, on_device(): jnp.dot(flat, whole_basis, preferred_element_type=jnp.float32)  2.87 us
  transfers between devices with their start and end apart: 10, of which 4 were waited for; matrix products, arithmetic and copies ran while one was open for 3% of the time, Pallas kernels for 0%

commit v1 on v0

--- a/solution.py
+++ b/solution.py
@@ -72,7 +72,18 @@
 def on_device(patterns, basis, valid, strength):
     cells_x, cells_y, pixels = patterns.shape
     flat = patterns.reshape(cells_x * cells_y, pixels)
-    whole_basis = lax.all_gather(basis, ("sx", "sy"), axis=1, tiled=True)
+    ways = lax.axis_size(("sx", "sy"))
+    up_2 = [(d, (d + 1) % ways) for d in range(ways)]
+    down_2 = [(d, (d - 1) % ways) for d in range(ways)]
+    earlier, later = ([basis], [basis])
+    for _ in range(ways // 2):
+        earlier.append(lax.ppermute(earlier[-1], ("sx", "sy"), up_2))
+    for _ in range((ways - 1) // 2):
+        later.append(lax.ppermute(later[-1], ("sx", "sy"), down_2))
+    line = jnp.concatenate([*earlier[::-1], *later[1:]], axis=1)
+    whole_basis = jnp.roll(
+        line, (lax.axis_index(("sx", "sy")) - ways // 2) * basis.shape[1], axis=1
+    )
     partial_value = jnp.dot(flat, whole_basis, preferred_element_type=jnp.float32)
     partial_value = partial_value.reshape(cells_x, cells_y, partial_value.shape[1])
     mask_full = valid.astype(jnp.float32)

time: 118 us -> 122 us (1.034)
  starting transfers between devices: 21.4 us -> 27.9 us
  waiting for transfers between devices: 64.1 us -> 60.4 us
  local copies, waits for them, and re-layouts: 2.33 us -> 5.85 us
  matrix products: 5.06 us -> 3 us
    all_gather x1 -> x0, waiting for transfers between devices: 28.3 us -> none  [on_device(): whole_basis = lax.all_gather(basis, ('sx', 'sy'), axis=1, tiled=True)]
    ppermute x0 -> x7, waiting for transfers between devices: none -> 22.3 us  [the longest x4 22 us: on_device(): earlier.append(lax.ppermute(earlier[-1], ('sx', 'sy'), up_2))]
    ppermute x0 -> x7, starting transfers between devices: none -> 7.96 us  [the longest x3 5.89 us: on_device(): later.append(lax.ppermute(later[-1], ('sx', 'sy'), down_2))]
    psum x1, waiting for transfers between devices: 28.8 us -> 32.8 us  [on_device(): coeffs = lax.psum(partial_value, 'px')]
    ppermute x4, starting transfers between devices: 14.9 us -> 12.3 us  [extended(): before = lax.ppermute(last, axis, up)]
    unnamed x12 -> x31, local copies, waits for them, and re-layouts: 1.19 us -> 3.69 us
    dot_general x1, matrix products: 2.87 us -> 0.8 us  [on_device(): jnp.dot(flat, whole_basis, preferred_element_type=jnp.float32)]
    ppermute x4, waiting for transfers between devices: 6.18 us -> 4.41 us  [extended(): after = lax.ppermute(initial, axis, down)]
  transfers between devices with their start and end apart: 10 -> 16, of which waited for: 4 -> 10; matrix products, arithmetic and copies ran while one was open for 3% -> 4% of each run, Pallas kernels for 0% -> 0%
where the time goes in v1:
time: 122 us
  waiting for transfers between devices  60.4 us (50%)
  starting transfers between devices  27.9 us (23%)
  between operations  13.8 us (11%)
  other arithmetic  11.1 us (9%)
  local copies, waits for them, and re-layouts  5.85 us (5%)
  matrix products  3 us (2%)
    psum x1, waiting for transfers between devices, on_device(): coeffs = lax.psum(partial_value, 'px')  32.8 us
    ppermute x4, waiting for transfers between devices, on_device(): earlier.append(lax.ppermute(earlier[-1], ('sx', 'sy'), up_2))  22 us
    ppermute x4, starting transfers between devices, extended(): before = lax.ppermute(last, axis, up)  12.3 us
    ppermute x4, starting transfers between devices, extended(): after = lax.ppermute(initial, axis, down)  7.6 us
    ppermute x3, starting transfers between devices, on_device(): later.append(lax.ppermute(later[-1], ('sx', 'sy'), down_2))  5.89 us
    convert_element_type x1, other arithmetic, on_device(): blend(coeffs, padded, mask_pad, gaps, strength).astype(jnp.bfloat16)  5.44 us
    reduce_sum x5, other arithmetic, squared_gaps(): gaps.append(jnp.sum(differ * differ, axis=-1))  5.38 us
    ppermute x4, waiting for transfers between devices, extended(): after = lax.ppermute(initial, axis, down)  4.41 us
  transfers between devices with their start and end apart: 16, of which 10 were waited for; matrix products, arithmetic and copies ran while one was open for 4% of the time, Pallas kernels for 0%

profile of v1, /device:TPU:1, one launch (start us, length us, event | category | flops | bytes accessed | tf_op | source)
XLA Modules:
  0.0 122.0 jit_solution(3688364553190930410)
XLA Ops:
  6.5 0.0 copy-start
  6.5 0.0 copy-start.4
  6.5 0.0 all-reduce.2.cloned.1.call-start
  6.5 2.1 %collective-permute-start = (bf16[2304,32]{0,1:T(8,128)(2,1)}, bf16[2304,32]{0,1:T(8,128)(2,1)S(1)}, u32[]{:S(2)}, u32[]{:S(2)}) collective-permute-start(bf16[2304,32]{0,1:T(8,128)(2,1)} %param.5), channel_id=1, source_target_pairs={{0,4},{4,8},{8,12},{12,16},{16,20},{20,24},{24,28},{28,0},{1,5},{5... | collective-permute-start | bytes 442376 | tf_op jit(solution)/shard_map/ppermute | solution.py:80
  8.6 5.2 %collective-permute-done = bf16[2304,32]{0,1:T(8,128)(2,1)S(1)} collective-permute-done((bf16[2304,32]{0,1:T(8,128)(2,1)}, bf16[2304,32]{0,1:T(8,128)(2,1)S(1)}, u32[]{:S(2)}, u32[]{:S(2)}) %collective-permute-start) | collective-permute-done | bytes 147488 | tf_op jit(solution)/shard_map/ppermute | solution.py:80
  13.8 0.0 collective-permute-start.1
  13.8 1.7 %collective-permute-start.4 = (bf16[2304,32]{0,1:T(8,128)(2,1)}, bf16[2304,32]{0,1:T(8,128)(2,1)S(1)}, u32[]{:S(2)}, u32[]{:S(2)}) collective-permute-start(bf16[2304,32]{0,1:T(8,128)(2,1)} %param.5), channel_id=1, source_target_pairs={{0,28},{4,0},{8,4},{12,8},{16,12},{20,16},{24,20},{28,24},{1,29},{... | collective-permute-start | bytes 442376 | tf_op jit(solution)/shard_map/ppermute | solution.py:82
  15.6 5.4 %collective-permute-done.1 = bf16[2304,32]{0,1:T(8,128)(2,1)S(1)} collective-permute-done((bf16[2304,32]{0,1:T(8,128)(2,1)S(1)}, bf16[2304,32]{0,1:T(8,128)(2,1)S(1)}, u32[]{:S(2)}, u32[]{:S(2)}) %collective-permute-start.1) | collective-permute-done | bytes 147488 | tf_op jit(solution)/shard_map/ppermute | solution.py:80
  21.0 0.0 collective-permute-start.2
  21.0 0.4 collective-permute-done.4
  21.4 1.9 %collective-permute-start.5 = (bf16[2304,32]{0,1:T(8,128)(2,1)S(1)}, bf16[2304,32]{0,1:T(8,128)(2,1)S(1)}, u32[]{:S(2)}, u32[]{:S(2)}) collective-permute-start(bf16[2304,32]{0,1:T(8,128)(2,1)S(1)} %collective-permute-done.4), channel_id=1, source_target_pairs={{0,28},{4,0},{8,4},{12,8},{16,12},{20,16},{24,20},{28,24},{1,29},{... | collective-permute-start | bytes 442376 | tf_op jit(solution)/shard_map/ppermute | solution.py:82
  23.3 5.5 %collective-permute-done.2 = bf16[2304,32]{0,1:T(8,128)(2,1)S(1)} collective-permute-done((bf16[2304,32]{0,1:T(8,128)(2,1)S(1)}, bf16[2304,32]{0,1:T(8,128)(2,1)S(1)}, u32[]{:S(2)}, u32[]{:S(2)}) %collective-permute-start.2) | collective-permute-done | bytes 147488 | tf_op jit(solution)/shard_map/ppermute | solution.py:80
  28.7 0.0 collective-permute-start.3
  28.7 0.0 collective-permute-done.5
  28.7 2.3 %collective-permute-start.6 = (bf16[2304,32]{0,1:T(8,128)(2,1)S(1)}, bf16[2304,32]{0,1:T(8,128)(2,1)S(1)}, u32[]{:S(2)}, u32[]{:S(2)}) collective-permute-start(bf16[2304,32]{0,1:T(8,128)(2,1)S(1)} %collective-permute-done.5), channel_id=1, source_target_pairs={{0,28},{4,0},{8,4},{12,8},{16,12},{20,16},{24,20},{28,24},{1,29},{... | collective-permute-start | bytes 442376 | tf_op jit(solution)/shard_map/ppermute | solution.py:82
  31.0 5.8 %collective-permute-done.3 = bf16[2304,32]{0,1:T(8,128)(2,1)S(1)} collective-permute-done((bf16[2304,32]{0,1:T(8,128)(2,1)S(1)}, bf16[2304,32]{0,1:T(8,128)(2,1)S(1)}, u32[]{:S(2)}, u32[]{:S(2)}) %collective-permute-start.3) | collective-permute-done | bytes 147488 | tf_op jit(solution)/shard_map/ppermute | solution.py:80
  36.9 0.9 constant_dynamic-update-slice_fusion.11
  37.9 0.0 collective-permute-done.6
  38.0 0.0 copy-done.4
  38.1 0.0 copy-done
  38.1 0.0 copy-start.2
  38.1 1.4 %copy-done.2 = bf16[2304,512]{0,1:T(8,128)(2,1)} copy-done((bf16[2304,512]{0,1:T(8,128)(2,1)}, bf16[2304,512]{0,1:T(8,128)(2,1)S(1)}, u32[]{:S(2)}) %copy-start.2) | copy-done | bytes 2359320
  39.5 0.0 copy-start.6
  39.5 0.8 convolution_bitcast_fusion
  40.3 1.0 copy.5
  41.3 0.0 all-reduce.2.cloned.1.call-update
  41.4 0.0 copy-done.6
  41.4 3.1 %collective-permute-start.8 = (f32[3,32]{1,0:T(4,128)S(1)}, f32[3,32]{1,0:T(4,128)S(1)}, u32[]{:S(2)}, u32[]{:S(2)}) collective-permute-start(f32[3,32]{1,0:T(4,128)S(1)} %get-tuple-element.125), channel_id=1, source_target_pairs={{8,0},{16,8},{24,16},{9,1},{17,9},{25,17},{10,2},{18,10},{26,18},{... | collective-permute-start | bytes 1160 | tf_op jit(solution)/shard_map/ppermute | solution.py:18
  44.5 2.4 %collective-permute-start.7 = (f32[3,32]{1,0:T(4,128)S(1)}, f32[3,32]{1,0:T(4,128)S(1)}, u32[]{:S(2)}, u32[]{:S(2)}) collective-permute-start(f32[3,32]{1,0:T(4,128)S(1)} %get-tuple-element.124), channel_id=1, source_target_pairs={{0,8},{8,16},{16,24},{1,9},{9,17},{17,25},{2,10},{10,18},{18,26},{... | collective-permute-start | bytes 1160 | tf_op jit(solution)/shard_map/ppermute | solution.py:17
  47.0 0.0 collective-permute-done.8
  47.0 0.7 collective-permute-done.7
  47.7 32.8 %all-reduce.2.cloned.1.call-done = f32[16,32,256]{2,1,0:T(8,128)} async-done(((f32[16,32,256]{2,1,0:T(8,128)}), f32[16,32,256]{2,1,0:T(8,128)}) %all-reduce.2.cloned.1.call-update) | async-done | bytes 524304 | tf_op jit(solution)/shard_map/psum | solution.py:90
  80.5 0.0 copy-start.1
  80.5 1.0 fusion.61
  81.5 4.6 %collective-permute-start.10 = (f32[3,32,256]{2,1,0:T(8,128)S(1)}, f32[3,32,256]{2,1,0:T(8,128)S(1)}, u32[]{:S(2)}, u32[]{:S(2)}) collective-permute-start(f32[3,32,256]{2,1,0:T(8,128)S(1)} %get-tuple-element.116), channel_id=1, source_target_pairs={{0,8},{8,16},{16,24},{1,9},{9,17},{17,25},{2,10},{10,18},{18,26},{... | collective-permute-start | bytes 294920 | tf_op jit(solution)/shard_map/ppermute | solution.py:17
  86.1 0.1 fusion.62
  86.1 1.3 %collective-permute-start.13 = (f32[22,3]{1,0:T(8,128)S(1)}, f32[22,3]{1,0:T(8,128)S(1)}, u32[]{:S(2)}, u32[]{:S(2)}) collective-permute-start(f32[22,3]{1,0:T(8,128)S(1)} %get-tuple-element.122), channel_id=1, source_target_pairs={{4,0},{5,1},{6,2},{7,3},{12,8},{13,9},{14,10},{15,11},{20,16},{21,... | collective-permute-start | bytes 800 | tf_op jit(solution)/shard_map/ppermute | solution.py:18
  87.4 4.0 %collective-permute-start.9 = (f32[22,3]{1,0:T(8,128)S(1)}, f32[22,3]{1,0:T(8,128)S(1)}, u32[]{:S(2)}, u32[]{:S(2)}) collective-permute-start(f32[22,3]{1,0:T(8,128)S(1)} %get-tuple-element.123), channel_id=1, source_target_pairs={{0,4},{1,5},{2,6},{3,7},{8,12},{9,13},{10,14},{11,15},{16,20},{17,... | collective-permute-start | bytes 800 | tf_op jit(solution)/shard_map/ppermute | solution.py:17
  91.4 1.9 %collective-permute-start.11 = (f32[3,32,256]{2,1,0:T(8,128)S(1)}, f32[3,32,256]{2,1,0:T(8,128)S(1)}, u32[]{:S(2)}, u32[]{:S(2)}) collective-permute-start(f32[3,32,256]{2,1,0:T(8,128)S(1)} %get-tuple-element.117), channel_id=1, source_target_pairs={{8,0},{16,8},{24,16},{9,1},{17,9},{25,17},{10,2},{18,10},{26,18},{... | collective-permute-start | bytes 294920 | tf_op jit(solution)/shard_map/ppermute | solution.py:18
  93.3 0.0 collective-permute-done.10
  93.4 1.2 constant_dynamic-update-slice_fusion.17
  94.5 2.8 %collective-permute-done.11 = f32[3,32,256]{2,1,0:T(8,128)S(1)} collective-permute-done((f32[3,32,256]{2,1,0:T(8,128)S(1)}, f32[3,32,256]{2,1,0:T(8,128)S(1)}, u32[]{:S(2)}, u32[]{:S(2)}) %collective-permute-start.11) | collective-permute-done | bytes 98336 | tf_op jit(solution)/shard_map/ppermute | solution.py:18
  97.4 1.3 %collective-permute-start.12 = (f32[22,3,256]{2,1,0:T(4,128)S(1)}, f32[22,3,256]{2,1,0:T(4,128)S(1)}, u32[]{:S(2)}, u32[]{:S(2)}) collective-permute-start(f32[22,3,256]{2,1,0:T(4,128)S(1)} %get-tuple-element.112), channel_id=1, source_target_pairs={{0,4},{1,5},{2,6},{3,7},{8,12},{9,13},{10,14},{11,15},{16,20},{17,... | collective-permute-start | bytes 202760 | tf_op jit(solution)/shard_map/ppermute | solution.py:17
  98.7 0.0 collective-permute-done.13
  98.7 0.0 collective-permute-done.9
  98.7 0.1 pad_maximum_fusion.3
  98.8 1.3 %collective-permute-start.14 = (f32[22,3,256]{2,1,0:T(4,128)S(1)}, f32[22,3,256]{2,1,0:T(4,128)S(1)}, u32[]{:S(2)}, u32[]{:S(2)}) collective-permute-start(f32[22,3,256]{2,1,0:T(4,128)S(1)} %get-tuple-element.111), channel_id=1, source_target_pairs={{4,0},{5,1},{6,2},{7,3},{12,8},{13,9},{14,10},{15,11},{20,16},{21,... | collective-permute-start | bytes 202760 | tf_op jit(solution)/shard_map/ppermute | solution.py:18
  100.1 0.1 collective-permute-done.12
  100.2 0.0 copy-done.1
  100.2 1.1 multiply_reduce_fusion.46
  101.4 1.1 multiply_reduce_fusion.47
  102.5 1.6 %collective-permute-done.14 = f32[22,3,256]{2,1,0:T(4,128)S(1)} collective-permute-done((f32[22,3,256]{2,1,0:T(4,128)S(1)}, f32[22,3,256]{2,1,0:T(4,128)S(1)}, u32[]{:S(2)}, u32[]{:S(2)}) %collective-permute-start.14) | collective-permute-done | bytes 67616 | tf_op jit(solution)/shard_map/ppermute | solution.py:18
  104.1 1.0 multiply_reduce_fusion.42
  105.1 1.0 multiply_reduce_fusion.43
  106.1 0.0 copy-start.5
  106.1 1.2 multiply_reduce_fusion.45
  107.3 0.0 copy-done.5
  107.3 0.2 add_add_fusion
  107.5 0.0 copy-start.3
  107.5 5.4 %divide_convert_fusion = bf16[16,32,256]{2,1,0:T(8,128)(2,1)S(1)} fusion(f32[16,32,256]{2,1,0:T(8,128)S(1)} %copy-done.1, f32[19,32,256]{2,1,0:T(8,128)S(1)} %constant_dynamic-update-slice_fusion.21, f32[19,32,256]{2,1,0:T(8,128)S(1)} %get-tuple-element.115, f32[22,32,256]{2,1,0:T(8,128)S(1)} %constant_dynamic-update-slice_fusion.16, ...), kind=kLoop, calls=%fused_computation.126 | loop fusion | flops 18350080 | bytes 4888576 | tf_op jit(solution)/shard_map/convert_element_type | solution.py:93
  113.0 0.0 copy-done.3
  113.0 2.2 %convolution_convert_fusion = bf16[512,2304]{1,0:T(8,128)(2,1)} fusion(bf16[512,256]{1,0:T(8,128)(2,1)S(1)} %bitcast.10, bf16[2304,512]{0,1:T(8,128)(2,1)S(1)} %copy-done.3, s32[]{:T(128)S(6)} %select_n.14), kind=kOutput, calls=%fused_computation.40 | convolution fusion | flops 605159424 | bytes 3801092 | tf_op jit(solution)/shard_map/dot_general | solution.py:95
  (22 shorter events, 0.3 us)
Async XLA Ops:
  6.5 31.6 %copy-start = (bf16[16,32,2304]{2,1,0:T(8,128)(2,1)S(1)}, bf16[16,32,2304]{2,1,0:T(8,128)(2,1)}, u32[]{:S(2)}) copy-start(bf16[16,32,2304]{2,1,0:T(8,128)(2,1)} %param.4) | copy-start | bytes 7077892
  6.5 31.5 %copy-start.4 = (bf16[2304,32]{0,1:T(8,128)(2,1)S(1)}, bf16[2304,32]{0,1:T(8,128)(2,1)}, u32[]{:S(2)}) copy-start(bf16[2304,32]{0,1:T(8,128)(2,1)} %param.5) | copy-start | bytes 442372
  6.5 73.9 %all-reduce.2.cloned.1.call-start = ((), (), s32[]{:S(2)}) async-start(), calls=%async_computation | async-start | bytes 1048576 | tf_op jit(solution)/shard_map/psum | solution.py:90
  6.5 7.3 %collective-permute-start = (bf16[2304,32]{0,1:T(8,128)(2,1)}, bf16[2304,32]{0,1:T(8,128)(2,1)S(1)}, u32[]{:S(2)}, u32[]{:S(2)}) collective-permute-start(bf16[2304,32]{0,1:T(8,128)(2,1)} %param.5), channel_id=1, source_target_pairs={{0,4},{4,8},{8,12},{12,16},{16,20},{20,24},{24,28},{28,0},{1,5},{5... | collective-permute-start | bytes 442376 | tf_op jit(solution)/shard_map/ppermute | solution.py:80
  13.8 7.2 %collective-permute-start.1 = (bf16[2304,32]{0,1:T(8,128)(2,1)S(1)}, bf16[2304,32]{0,1:T(8,128)(2,1)S(1)}, u32[]{:S(2)}, u32[]{:S(2)}) collective-permute-start(bf16[2304,32]{0,1:T(8,128)(2,1)S(1)} %collective-permute-done), channel_id=1, source_target_pairs={{0,4},{4,8},{8,12},{12,16},{16,20},{20,24},{24,28},{28,0},{1,5},{5... | collective-permute-start | bytes 442376 | tf_op jit(solution)/shard_map/ppermute | solution.py:80
  13.8 7.6 %collective-permute-start.4 = (bf16[2304,32]{0,1:T(8,128)(2,1)}, bf16[2304,32]{0,1:T(8,128)(2,1)S(1)}, u32[]{:S(2)}, u32[]{:S(2)}) collective-permute-start(bf16[2304,32]{0,1:T(8,128)(2,1)} %param.5), channel_id=1, source_target_pairs={{0,28},{4,0},{8,4},{12,8},{16,12},{20,16},{24,20},{28,24},{1,29},{... | collective-permute-start | bytes 442376 | tf_op jit(solution)/shard_map/ppermute | solution.py:82
  21.0 7.8 %collective-permute-start.2 = (bf16[2304,32]{0,1:T(8,128)(2,1)S(1)}, bf16[2304,32]{0,1:T(8,128)(2,1)S(1)}, u32[]{:S(2)}, u32[]{:S(2)}) collective-permute-start(bf16[2304,32]{0,1:T(8,128)(2,1)S(1)} %collective-permute-done.1), channel_id=1, source_target_pairs={{0,4},{4,8},{8,12},{12,16},{16,20},{20,24},{24,28},{28,0},{1,5},{5... | collective-permute-start | bytes 442376 | tf_op jit(solution)/shard_map/ppermute | solution.py:80
  21.4 7.4 %collective-permute-start.5 = (bf16[2304,32]{0,1:T(8,128)(2,1)S(1)}, bf16[2304,32]{0,1:T(8,128)(2,1)S(1)}, u32[]{:S(2)}, u32[]{:S(2)}) collective-permute-start(bf16[2304,32]{0,1:T(8,128)(2,1)S(1)} %collective-permute-done.4), channel_id=1, source_target_pairs={{0,28},{4,0},{8,4},{12,8},{16,12},{20,16},{24,20},{28,24},{1,29},{... | collective-permute-start | bytes 442376 | tf_op jit(solution)/shard_map/ppermute | solution.py:82
  28.7 8.1 %collective-permute-start.3 = (bf16[2304,32]{0,1:T(8,128)(2,1)S(1)}, bf16[2304,32]{0,1:T(8,128)(2,1)S(1)}, u32[]{:S(2)}, u32[]{:S(2)}) collective-permute-start(bf16[2304,32]{0,1:T(8,128)(2,1)S(1)} %collective-permute-done.2), channel_id=1, source_target_pairs={{0,4},{4,8},{8,12},{12,16},{16,20},{20,24},{24,28},{28,0},{1,5},{5... | collective-permute-start | bytes 442376 | tf_op jit(solution)/shard_map/ppermute | solution.py:80
  28.7 9.1 %collective-permute-start.6 = (bf16[2304,32]{0,1:T(8,128)(2,1)S(1)}, bf16[2304,32]{0,1:T(8,128)(2,1)S(1)}, u32[]{:S(2)}, u32[]{:S(2)}) collective-permute-start(bf16[2304,32]{0,1:T(8,128)(2,1)S(1)} %collective-permute-done.5), channel_id=1, source_target_pairs={{0,28},{4,0},{8,4},{12,8},{16,12},{20,16},{24,20},{28,24},{1,29},{... | collective-permute-start | bytes 442376 | tf_op jit(solution)/shard_map/ppermute | solution.py:82
  38.1 1.4 %copy-start.2 = (bf16[2304,512]{0,1:T(8,128)(2,1)}, bf16[2304,512]{0,1:T(8,128)(2,1)S(1)}, u32[]{:S(2)}) copy-start(bf16[2304,512]{0,1:T(8,128)(2,1)S(1)} %constant_dynamic-update-slice_fusion) | copy-start | bytes 7077892
  39.5 1.9 %copy-start.6 = (s32[16,32]{1,0:T(8,128)S(1)}, s32[16,32]{1,0:T(8,128)}, u32[]{:S(2)}) copy-start(s32[16,32]{1,0:T(8,128)} %param.6) | copy-start | bytes 6148
  41.4 5.6 %collective-permute-start.8 = (f32[3,32]{1,0:T(4,128)S(1)}, f32[3,32]{1,0:T(4,128)S(1)}, u32[]{:S(2)}, u32[]{:S(2)}) collective-permute-start(f32[3,32]{1,0:T(4,128)S(1)} %get-tuple-element.125), channel_id=1, source_target_pairs={{8,0},{16,8},{24,16},{9,1},{17,9},{25,17},{10,2},{18,10},{26,18},{... | collective-permute-start | bytes 1160 | tf_op jit(solution)/shard_map/ppermute | solution.py:18
  44.5 3.2 %collective-permute-start.7 = (f32[3,32]{1,0:T(4,128)S(1)}, f32[3,32]{1,0:T(4,128)S(1)}, u32[]{:S(2)}, u32[]{:S(2)}) collective-permute-start(f32[3,32]{1,0:T(4,128)S(1)} %get-tuple-element.124), channel_id=1, source_target_pairs={{0,8},{8,16},{16,24},{1,9},{9,17},{17,25},{2,10},{10,18},{18,26},{... | collective-permute-start | bytes 1160 | tf_op jit(solution)/shard_map/ppermute | solution.py:17
  80.5 19.8 %copy-start.1 = (f32[16,32,256]{2,1,0:T(8,128)S(1)}, f32[16,32,256]{2,1,0:T(8,128)}, u32[]{:S(2)}) copy-start(f32[16,32,256]{2,1,0:T(8,128)} %all-reduce.2.cloned.1.call-done) | copy-start | bytes 1572868
  81.5 11.9 %collective-permute-start.10 = (f32[3,32,256]{2,1,0:T(8,128)S(1)}, f32[3,32,256]{2,1,0:T(8,128)S(1)}, u32[]{:S(2)}, u32[]{:S(2)}) collective-permute-start(f32[3,32,256]{2,1,0:T(8,128)S(1)} %get-tuple-element.116), channel_id=1, source_target_pairs={{0,8},{8,16},{16,24},{1,9},{9,17},{17,25},{2,10},{10,18},{18,26},{... | collective-permute-start | bytes 294920 | tf_op jit(solution)/shard_map/ppermute | solution.py:17
  86.1 12.6 %collective-permute-start.13 = (f32[22,3]{1,0:T(8,128)S(1)}, f32[22,3]{1,0:T(8,128)S(1)}, u32[]{:S(2)}, u32[]{:S(2)}) collective-permute-start(f32[22,3]{1,0:T(8,128)S(1)} %get-tuple-element.122), channel_id=1, source_target_pairs={{4,0},{5,1},{6,2},{7,3},{12,8},{13,9},{14,10},{15,11},{20,16},{21,... | collective-permute-start | bytes 800 | tf_op jit(solution)/shard_map/ppermute | solution.py:18
  87.4 11.3 %collective-permute-start.9 = (f32[22,3]{1,0:T(8,128)S(1)}, f32[22,3]{1,0:T(8,128)S(1)}, u32[]{:S(2)}, u32[]{:S(2)}) collective-permute-start(f32[22,3]{1,0:T(8,128)S(1)} %get-tuple-element.123), channel_id=1, source_target_pairs={{0,4},{1,5},{2,6},{3,7},{8,12},{9,13},{10,14},{11,15},{16,20},{17,... | collective-permute-start | bytes 800 | tf_op jit(solution)/shard_map/ppermute | solution.py:17
  91.4 5.9 %collective-permute-start.11 = (f32[3,32,256]{2,1,0:T(8,128)S(1)}, f32[3,32,256]{2,1,0:T(8,128)S(1)}, u32[]{:S(2)}, u32[]{:S(2)}) collective-permute-start(f32[3,32,256]{2,1,0:T(8,128)S(1)} %get-tuple-element.117), channel_id=1, source_target_pairs={{8,0},{16,8},{24,16},{9,1},{17,9},{25,17},{10,2},{18,10},{26,18},{... | collective-permute-start | bytes 294920 | tf_op jit(solution)/shard_map/ppermute | solution.py:18
  97.4 2.8 %collective-permute-start.12 = (f32[22,3,256]{2,1,0:T(4,128)S(1)}, f32[22,3,256]{2,1,0:T(4,128)S(1)}, u32[]{:S(2)}, u32[]{:S(2)}) collective-permute-start(f32[22,3,256]{2,1,0:T(4,128)S(1)} %get-tuple-element.112), channel_id=1, source_target_pairs={{0,4},{1,5},{2,6},{3,7},{8,12},{9,13},{10,14},{11,15},{16,20},{17,... | collective-permute-start | bytes 202760 | tf_op jit(solution)/shard_map/ppermute | solution.py:17
  98.8 5.3 %collective-permute-start.14 = (f32[22,3,256]{2,1,0:T(4,128)S(1)}, f32[22,3,256]{2,1,0:T(4,128)S(1)}, u32[]{:S(2)}, u32[]{:S(2)}) collective-permute-start(f32[22,3,256]{2,1,0:T(4,128)S(1)} %get-tuple-element.111), channel_id=1, source_target_pairs={{4,0},{5,1},{6,2},{7,3},{12,8},{13,9},{14,10},{15,11},{20,16},{21,... | collective-permute-start | bytes 202760 | tf_op jit(solution)/shard_map/ppermute | solution.py:18
  106.1 1.2 copy-start.5
  107.5 5.5 %copy-start.3 = (bf16[2304,512]{0,1:T(8,128)(2,1)S(1)}, bf16[2304,512]{0,1:T(8,128)(2,1)}, u32[]{:S(2)}) copy-start(bf16[2304,512]{0,1:T(8,128)(2,1)} %copy-done.2) | copy-start | bytes 7077892
Sparse Core Ops, SparseCore 0:
  41.5 38.9 all-reduce.1
